TPU v7x, 32 devices: a whole 2x2x4 slice. The times are simulated.
32 devices in a mesh: band: 8 (over y, x, core), ga: 4 (over z).
Axes of the slice: x: 2, y: 2, z: 4, core: 2. Of those that a mesh axis runs over, the one named last changes fastest.
Arguments:
- orbitals: bfloat16 [256, 90112], P(('band', 'ga')), may hold values from -6 to 6
- local_part: bfloat16 [256, 90112], P(('band', 'ga')), may hold values from -6 to 6
- projectors: bfloat16 [90112, 1664], P(('band', 'ga')), may hold values from -0.01953125 to 0.01953125
- couplings: float32 [4, 13, 13], replicated, may hold values from -20 to 20, as said below
- species: int32 [128], replicated, may hold values from 0 to 3
Outputs:
- applied: bfloat16 [256, 90112], P(('band', 'ga'))
Inputs may be any that keep to these rules, and one draw needn't show every extreme that they name: `couplings`: each species has one symmetric block.
All inputs are finite; a program needn't handle non-finite values.
Results may differ from a plain program's by a relative error of at most 0.0056.
Values may be sent and summed in bfloat16 or wider, within the bound.
A program may use at most 64 MiB of HBM per device.

v0:
```python
import jax
import jax.numpy as jnp
from jax import lax
from jax.sharding import PartitionSpec as P


def select_blocks(couplings, species):
    kinds = couplings.shape[0]
    width = couplings.shape[1]
    select = (jnp.arange(kinds, dtype=jnp.int32)[:, None] == species[None, :]).astype(jnp.float32)
    table = jnp.einsum(
        "sk,sa->ka",
        couplings.reshape(kinds, width * width),
        select,
        precision=lax.Precision.HIGHEST,
    )
    return table.reshape(width, width, species.shape[0])


def couple(totals, blocks):
    width = blocks.shape[0]
    atom_count = blocks.shape[2]
    folded = totals.reshape(totals.shape[0], width, atom_count)
    mixed = jnp.zeros_like(folded)
    for inner in range(width):
        mixed = mixed + folded[:, inner, None, :] * blocks[None, inner, :, :]
    return mixed.reshape(totals.shape[0], width * atom_count).astype(jnp.bfloat16)


def expand(coefs, projectors):
    return jnp.einsum("bp,gp->bg", coefs, projectors, preferred_element_type=jnp.float32).astype(
        jnp.bfloat16
    )


def on_device(orbitals, local_part, projectors, couplings, species):
    blocks = select_blocks(couplings, species)
    slab_orbitals = lax.all_to_all(
        orbitals, ("band", "ga"), split_axis=1, concat_axis=0, tiled=True
    )
    partial_value = jnp.dot(slab_orbitals, projectors, preferred_element_type=jnp.float32)
    totals = lax.psum(partial_value, ("band", "ga"))
    slab_correction = expand(couple(totals, blocks), projectors)
    correction = lax.all_to_all(
        slab_correction, ("band", "ga"), split_axis=0, concat_axis=1, tiled=True
    )
    correction = lax.optimization_barrier(correction)
    return (local_part.astype(jnp.float32) + correction.astype(jnp.float32)).astype(jnp.bfloat16)


def solution(mesh):
    placed = (P(("band", "ga"), None), P(("band", "ga"), None), P(("band", "ga"), None), P(), P())
    return jax.shard_map(
        on_device, mesh=mesh, in_specs=placed, out_specs=P(("band", "ga"), None), check_vma=False
    )
```

profile of v0, /device:TPU:8, one launch (start us, length us, event | category | flops | bytes accessed | tf_op | source)
XLA Modules:
  0.0 245.6 jit_solution(7646724141969409436)
XLA Ops:
  6.5 0.0 all-reduce.2.cloned.1.call-start
  6.5 40.7 %all_to_all.38 = bf16[8,32,2816]{2,0,1:T(8,128)(2,1)S(1)} all-to-all(bf16[8,32,2816]{2,0,1:T(8,128)(2,1)} %bitcast.148), channel_id=1, replica_groups=mesh['band'=8,'ga'=4] {'band','ga'}, dimensions={1} | all-to-all | bytes 2883584 | tf_op jit(solution)/shard_map/all_to_all | solution.py:38
  47.3 8.6 %fusion.14 = f32[256,1664]{0,1:T(8,128)} fusion(bf16[2816,1664]{1,0:T(8,128)(2,1)} %param.7, bf16[8,32,2816]{2,0,1:T(8,128)(2,1)S(1)} %all_to_all.38), kind=kOutput, calls=%fused_computation.29 | convolution fusion | flops 2399141888 | bytes 12517376 | tf_op jit(solution)/shard_map/dot_general | solution.py:41
  55.9 0.0 copy-start.1
  55.9 0.0 copy-start.2
  55.9 0.0 all-reduce.2.cloned.1.call-update
  55.9 0.7 copy-done.1
  56.7 0.1 reshape.81
  56.7 0.0 copy-done.2
  56.8 0.3 convolution_bitcast_fusion
  57.0 130.7 %all-reduce.2.cloned.1.call-done = f32[256,13,128]{0,2,1:T(8,128)} async-done(((f32[256,13,128]{0,2,1:T(8,128)}), f32[256,13,128]{0,2,1:T(8,128)}) %all-reduce.2.cloned.1.call-update) | async-done | bytes 1703952 | tf_op jit(solution)/shard_map/psum | solution.py:42
  187.7 1.6 slice_bitcast_fusion.12
  189.3 3.0 %fusion.2 = bf16[256,1664]{0,1:T(8,128)(2,1)S(1)} fusion(f32[1664]{0:T(1024)S(1)} %get-tuple-element.19, f32[256,128]{0,1:T(8,128)S(1)} %get-tuple-element.6, f32[1664]{0:T(1024)S(1)} %get-tuple-element.20, f32[256,128]{0,1:T(8,128)S(1)} %get-tuple-element.7, f32[1664]{0:T(1024)S(1)} %get-tuple-element.21, f32[256,128]{0,1:T(8,128)S(1)} %get-tuple-element.8, ...), kind=kLoop, calls=%fused_computation.5 | loop fusion | flops 11075584 | bytes 2642432 | tf_op jit(solution)/shard_map/convert_element_type | solution.py:27
  192.3 6.6 %fusion = bf16[32,8,2816]{2,1,0:T(8,128)(2,1)S(1)} fusion(bf16[256,1664]{0,1:T(8,128)(2,1)S(1)} %fusion.2, bf16[2816,1664]{1,0:T(8,128)(2,1)} %param.7), kind=kOutput, calls=%fused_computation.1 | convolution fusion | flops 2399862784 | bytes 11665408 | tf_op jit(solution)/shard_map/bp,gp->bg/dot_general | solution.py:31
  198.9 0.0 copy-start
  198.9 38.4 %all_to_all.39 = bf16[32,8,2816]{2,1,0:T(8,128)(2,1)S(1)} all-to-all(bf16[32,8,2816]{2,1,0:T(8,128)(2,1)S(1)} %fusion), channel_id=1, replica_groups=mesh['band'=8,'ga'=4] {'band','ga'}, dimensions={0} | all-to-all | bytes 2883584 | tf_op jit(solution)/shard_map/all_to_all | solution.py:44
  237.3 0.0 copy-done
  237.3 1.4 add_convert_fusion
  (2 shorter events, 0.0 us)
Async XLA Ops:
  6.5 181.2 %all-reduce.2.cloned.1.call-start = ((), (), s32[]{:S(2)}) async-start(), calls=%async_computation.2 | async-start | bytes 3407872 | tf_op jit(solution)/shard_map/psum | solution.py:42
  55.9 0.7 copy-start.1
  55.9 0.8 copy-start.2
  198.9 38.4 %copy-start = (bf16[8,90112]{1,0:T(8,128)(2,1)S(1)}, bf16[8,90112]{1,0:T(8,128)(2,1)}, u32[]{:S(2)}) copy-start(bf16[8,90112]{1,0:T(8,128)(2,1)} %param.6) | copy-start | bytes 4325380
Sparse Core Ops, SparseCore 0:
  56.1 131.6 all-reduce.1
where the time goes:
time: 248 us; the launch traced here: 246 us
  waiting for transfers between devices  131 us (53%)
  blocking collectives  79.1 us (32%)
  matrix products  15.5 us (6%)
  between operations  13.4 us (5%)
  other arithmetic  4.41 us (2%)
    psum x1, waiting for transfers between devices, on_device(): totals = lax.psum(partial_value, ('band', 'ga'))  131 us
    all_to_all x1, blocking collectives, on_device(): lax.all_to_all(orbitals, ('band', 'ga'), split_axis=1, concat_axis=0, til...  40.7 us
    all_to_all x1, blocking collectives, on_device(): lax.all_to_all(slab_correction, ('band', 'ga'), split_axis=0, concat_axis...  38.4 us
    dot_general x1, matrix products, on_device(): jnp.dot(slab_orbitals, projectors, preferred_element_type=jnp.float32)  8.63 us
    dot_general x1, matrix products, expand(): jnp.einsum('bp,gp->bg', coefs, projectors, preferred_element_type=jnp.flo...  6.57 us
  transfers between devices with their start and end apart: 1, of which 1 were waited for; matrix products, arithmetic and copies ran while one was open for 0% of the time, Pallas kernels for 0%

commit v1 on v0

--- a/solution.py
+++ b/solution.py
@@ -39,8 +39,14 @@
         orbitals, ("band", "ga"), split_axis=1, concat_axis=0, tiled=True
     )
     partial_value = jnp.dot(slab_orbitals, projectors, preferred_element_type=jnp.float32)
-    totals = lax.psum(partial_value, ("band", "ga"))
-    slab_correction = expand(couple(totals, blocks), projectors)
+    devices = lax.axis_size(("band", "ga"))
+    pieces = lax.all_to_all(
+        partial_value.astype(jnp.bfloat16), ("band", "ga"), split_axis=0, concat_axis=0, tiled=True
+    )
+    pieces = pieces.reshape(devices, pieces.shape[0] // devices, pieces.shape[1])
+    totals = jnp.sum(pieces.astype(jnp.float32), axis=0)
+    coefs = lax.all_gather(couple(totals, blocks), ("band", "ga"), axis=0, tiled=True)
+    slab_correction = expand(coefs, projectors)
     correction = lax.all_to_all(
         slab_correction, ("band", "ga"), split_axis=0, concat_axis=1, tiled=True
     )

time: 248 us -> 193 us (0.78)
  waiting for transfers between devices: 131 us -> 21.6 us
  blocking collectives: 79.1 us -> 150 us
  between operations: 13.4 us -> 0.08 us
  starting transfers between devices: 0.01 us -> 3.43 us
  other arithmetic: 4.41 us -> 1.62 us
    psum x1 -> x0, waiting for transfers between devices: 131 us -> none  [on_device(): totals = lax.psum(partial_value, ('band', 'ga'))]
    all_gather x0 -> x1, blocking collectives: none -> 69.7 us  [on_device(): lax.all_gather(couple(totals, blocks), ('band', 'ga'), axis=0, tiled=True)]
    all_to_all x0 -> x1, waiting for transfers between devices: none -> 21.6 us  [on_device(): lax.all_to_all(partial_value.astype(jnp.bfloat16), ('band', 'ga'), split_...]
    all_to_all x0 -> x1, starting transfers between devices: none -> 3.43 us  [on_device(): lax.all_to_all(partial_value.astype(jnp.bfloat16), ('band', 'ga'), split_...]
    convert_element_type x1, other arithmetic: 2.98 us -> 0.07 us  [couple(): mixed.reshape(totals.shape[0], width * atom_count).astype(jnp.bfloat16)]
where the time goes in v1:
time: 193 us; the launch traced here: 191 us
  blocking collectives  150 us (78%)
  waiting for transfers between devices  21.6 us (11%)
  matrix products  14.1 us (7%)
  starting transfers between devices  3.43 us (2%)
    all_gather x1, blocking collectives, on_device(): lax.all_gather(couple(totals, blocks), ('band', 'ga'), axis=0, tiled=True)  69.7 us
    all_to_all x1, blocking collectives, on_device(): lax.all_to_all(orbitals, ('band', 'ga'), split_axis=1, concat_axis=0, til...  40.7 us
    all_to_all x1, blocking collectives, on_device(): lax.all_to_all(slab_correction, ('band', 'ga'), split_axis=0, concat_axis...  39.4 us
    all_to_all x1, waiting for transfers between devices, on_device(): lax.all_to_all(partial_value.astype(jnp.bfloat16), ('band', 'ga'), split_...  21.6 us
    dot_general x1, matrix products, on_device(): jnp.dot(slab_orbitals, projectors, preferred_element_type=jnp.float32)  7.35 us
    dot_general x1, matrix products, expand(): jnp.einsum('bp,gp->bg', coefs, projectors, preferred_element_type=jnp.flo...  6.5 us
  transfers between devices with their start and end apart: 1, of which 1 were waited for; matrix products, arithmetic and copies ran while one was open for 0% of the time, Pallas kernels for 0%

profile of v1, /device:TPU:8, one launch (start us, length us, event | category | flops | bytes accessed | tf_op | source)
XLA Modules:
  0.0 190.9 jit_solution(15892471655889466248)
XLA Ops:
  0.0 40.7 %all_to_all.47 = bf16[8,32,2816]{2,0,1:T(8,128)(2,1)S(1)} all-to-all(bf16[8,32,2816]{2,0,1:T(8,128)(2,1)} %bitcast.149), channel_id=1, replica_groups=mesh['band'=8,'ga'=4] {'band','ga'}, dimensions={1} | all-to-all | bytes 2883584 | tf_op jit(solution)/shard_map/all_to_all | solution.py:38
  40.7 7.3 %fusion.1 = bf16[32,8,1664]{2,1,0:T(8,128)(2,1)} fusion(bf16[2816,1664]{1,0:T(8,128)(2,1)} %param.7, bf16[8,32,2816]{2,0,1:T(8,128)(2,1)S(1)} %all_to_all.47), kind=kOutput, calls=%fused_computation.4 | convolution fusion | flops 2399567872 | bytes 11665408 | tf_op jit(solution)/shard_map/dot_general | solution.py:41
  48.1 0.0 copy-start.1
  48.1 0.0 copy-start.2
  48.1 3.4 %all-to-all-start.1 = ((bf16[32,8,1664]{2,1,0:T(8,128)(2,1)}), bf16[32,8,1664]{2,1,0:T(8,128)(2,1)S(1)}, u32[]{:S(2)}, u32[]{:S(2)}) async-start(bf16[32,8,1664]{2,1,0:T(8,128)(2,1)} %fusion.1), calls=%async_computation.1 | async-start | bytes 1703936 | tf_op jit(solution)/shard_map/all_to_all | solution.py:43
  51.5 0.0 copy-done.1
  51.6 0.1 reshape.85
  51.6 0.0 copy-done.2
  51.7 0.3 convolution_bitcast_fusion
  51.9 21.6 %all-to-all-done.1 = bf16[32,8,1664]{2,1,0:T(8,128)(2,1)S(1)} async-done(((bf16[32,8,1664]{2,1,0:T(8,128)(2,1)}), bf16[32,8,1664]{2,1,0:T(8,128)(2,1)S(1)}, u32[]{:S(2)}, u32[]{:S(2)}) %all-to-all-start.1) | async-done | bytes 852000 | tf_op jit(solution)/shard_map/all_to_all | solution.py:43
  73.6 0.1 convert_reduce_fusion
  73.7 0.1 fusion.4
  73.8 69.7 %all_gather.3 = bf16[256,1664]{1,0:T(8,128)(2,1)S(1)} all-gather(bf16[8,1664]{1,0:T(8,128)(2,1)S(1)} %fusion.4), channel_id=1, replica_groups=mesh['band'=8,'ga'=4] {'band','ga'}, dimensions={0}, use_global_device_ids=true | all-gather | bytes 878592 | tf_op jit(solution)/shard_map/all_gather | solution.py:48
  143.5 6.5 %fusion = bf16[32,8,2816]{2,1,0:T(8,128)(2,1)S(1)} fusion(bf16[256,1664]{1,0:T(8,128)(2,1)S(1)} %all_gather.3, bf16[2816,1664]{1,0:T(8,128)(2,1)} %param.7), kind=kOutput, calls=%fused_computation.1 | convolution fusion | flops 2399862784 | bytes 11665408 | tf_op jit(solution)/shard_map/bp,gp->bg/dot_general | solution.py:31
  150.0 0.0 copy-start
  150.0 39.4 %all_to_all.48 = bf16[32,8,2816]{2,1,0:T(8,128)(2,1)S(1)} all-to-all(bf16[32,8,2816]{2,1,0:T(8,128)(2,1)S(1)} %fusion), channel_id=1, replica_groups=mesh['band'=8,'ga'=4] {'band','ga'}, dimensions={0} | all-to-all | bytes 2883584 | tf_op jit(solution)/shard_map/all_to_all | solution.py:50
  189.5 0.0 copy-done
  189.5 1.4 add_convert_fusion
  (3 shorter events, 0.0 us)
Async XLA Ops:
  48.1 3.4 %copy-start.1 = (f32[4,13,13]{2,0,1:T(4,128)S(1)}, f32[4,13,13]{2,0,1:T(4,128)}, u32[]{:S(2)}) copy-start(f32[4,13,13]{2,0,1:T(4,128)} %param.8) | copy-start | bytes 8116
  48.1 3.6 %copy-start.2 = (s32[128]{0:T(128)S(1)}, s32[128]{0:T(128)}, u32[]{:S(2)}) copy-start(s32[128]{0:T(128)} %param.9) | copy-start | bytes 1540
  48.1 25.5 %all-to-all-start.1 = ((bf16[32,8,1664]{2,1,0:T(8,128)(2,1)}), bf16[32,8,1664]{2,1,0:T(8,128)(2,1)S(1)}, u32[]{:S(2)}, u32[]{:S(2)}) async-start(bf16[32,8,1664]{2,1,0:T(8,128)(2,1)} %fusion.1), calls=%async_computation.1 | async-start | bytes 1703936 | tf_op jit(solution)/shard_map/all_to_all | solution.py:43
  150.0 39.4 %copy-start = (bf16[8,90112]{1,0:T(8,128)(2,1)S(1)}, bf16[8,90112]{1,0:T(8,128)(2,1)}, u32[]{:S(2)}) copy-start(bf16[8,90112]{1,0:T(8,128)(2,1)} %param.6) | copy-start | bytes 4325380
